TPU v7x, 256 devices: a whole 4x4x8 slice. The times are simulated.
256 devices in a mesh: client: 16 (over y_lo, z), tensor: 8 (over x, core), sdata: 2 (over y_hi).
Axes of the slice: x: 4, y: 4 (y_hi: 2, y_lo: 2; y = y_hi * 2 + y_lo), z: 8, core: 2. Of those that a mesh axis runs over, the one named last changes fastest.
Arguments:
- client_input: bfloat16 [12288, 2048], P(('client', 'sdata')), may hold values from -6 to 6
- client_gain: bfloat16 [16, 2048], P('client'), may hold values from 0.5 to 1.5
- query_weight: bfloat16 [16, 2048, 2048], P('client', None, 'tensor'), as said below
- key_weight: bfloat16 [16, 2048, 512], P('client', None, 'tensor'), as said below
- client_value_weight: bfloat16 [16, 2048, 512], P('client', None, 'tensor'), may hold values from -0.125 to 0.125
- output_weight: bfloat16 [16, 2048, 2048], P('client', None, 'tensor'), may hold values from -0.125 to 0.125
- server_gain: bfloat16 [2, 2048], P('sdata'), may hold values from 0.5 to 1.5
- server_gate: bfloat16 [2, 2048, 4096], P('sdata', None, 'tensor'), may hold values from -0.125 to 0.125
- server_up: bfloat16 [2, 2048, 4096], P('sdata', None, 'tensor'), may hold values from -0.125 to 0.125
- server_down: bfloat16 [2, 4096, 2048], P('sdata', 'tensor'), may hold values from -0.09375 to 0.09375
- upstream: bfloat16 [12288, 2048], P(('client', 'sdata')), may hold values from -6 to 6
- assignment: int32 [16], replicated, may hold values from 0 to 1, as said below
Outputs:
- query_update: bfloat16 [2048, 2048], P(('client', 'sdata'), 'tensor')
- key_update: bfloat16 [2048, 512], P(('client', 'sdata'), 'tensor')
- value_update: bfloat16 [2048, 512], P(('client', 'sdata'), 'tensor')
- output_update: bfloat16 [2048, 2048], P(('client', 'sdata'), 'tensor')
Inputs may be any that keep to these rules, and one draw needn't show every extreme that they name: `assignment`: each of the 2 server groups is named by exactly 8 clients. `query_weight`: independent entries with a spread of about 2048 ** -0.5. `key_weight`: entries with a spread of about 2048 ** -0.5 or more.
All inputs are finite; a program needn't handle non-finite values.
Results may differ from a plain program's by a relative error of at most 0.038.
The roundings to bfloat16 on the way count: a program that leaves them out, or rounds other values in their place, can miss the bound.
Values may be sent and summed in bfloat16 or wider, within the bound.
No kernel may reach another device: no remote copies, remote signals or barrier semaphores. Data moves between devices by JAX's collectives and lax.ppermute only.
A program may use at most 128 MiB of HBM per device.

v0:
```python
from functools import partial
import math
import jax
import jax.numpy as jnp
from jax import lax
from jax.sharding import PartitionSpec as P

HEAD_DIM = 64


def cut_along(value, dim, length):
    before, after = (value.shape[:dim], value.shape[dim + 1 :])
    return jnp.moveaxis(value.reshape(*before, length, -1, *after), dim, 0)


def sum_at_owner(value, axis, dim):
    length = lax.axis_size(axis)
    tiles = lax.all_to_all(cut_along(value, dim, length), axis, 0, 0, tiled=True)
    return jnp.sum(tiles.astype(jnp.float32), axis=0)


def rotary_tables(length):
    halfway = HEAD_DIM // 2
    positions = jnp.arange(length).astype(jnp.float32)
    exponents = jnp.arange(halfway).astype(jnp.float32) * (2.0 / HEAD_DIM)
    frequencies = jnp.exp(-math.log(500000.0) * exponents)
    angles = positions[:, None] * frequencies[None, :]
    cosine_table = jnp.concatenate([jnp.cos(angles), jnp.cos(angles)], 1)
    sine_table = jnp.concatenate([jnp.sin(angles), jnp.sin(angles)], 1)
    return (cosine_table, sine_table)


def rotary(heads_in, cosine_table, sine_table):
    halfway = heads_in.shape[-1] // 2
    turned = jnp.concatenate([-heads_in[..., halfway:], heads_in[..., :halfway]], -1)
    return heads_in * cosine_table[:, None, :] + turned * sine_table[:, None, :]


def normalize(rows_in, gain):
    rows_float = rows_in.astype(jnp.float32)
    inv_rms = lax.rsqrt(jnp.mean(rows_float * rows_float, -1, keepdims=True) + 1e-05)
    return (rows_float * inv_rms * gain.astype(jnp.float32)).astype(jnp.bfloat16)


def attention_part(normed, query_matrix, client_key_matrix, value_matrix, output_matrix):
    length = normed.shape[0]
    query_count = query_matrix.shape[1] // HEAD_DIM
    shared_count = client_key_matrix.shape[1] // HEAD_DIM
    group_size = query_count // shared_count
    cosine_table, sine_table = rotary_tables(length)
    queries = jnp.dot(normed, query_matrix, preferred_element_type=jnp.float32).reshape(
        length, query_count, HEAD_DIM
    )
    queries = (
        rotary(queries, cosine_table, sine_table)
        .astype(jnp.bfloat16)
        .reshape(length, shared_count, group_size, HEAD_DIM)
    )
    key_heads = jnp.dot(normed, client_key_matrix, preferred_element_type=jnp.float32).reshape(
        length, shared_count, HEAD_DIM
    )
    key_heads = rotary(key_heads, cosine_table, sine_table).astype(jnp.bfloat16)
    value_heads = (
        jnp.dot(normed, value_matrix, preferred_element_type=jnp.float32)
        .astype(jnp.bfloat16)
        .reshape(length, shared_count, HEAD_DIM)
    )
    scores = jnp.einsum(
        "qgrd,kgd->grqk", queries.astype(jnp.float32), key_heads.astype(jnp.float32)
    ) * HEAD_DIM ** (-0.5)
    row_ids = lax.broadcasted_iota(jnp.int32, (length, length), 0)
    col_ids = lax.broadcasted_iota(jnp.int32, (length, length), 1)
    scores = jnp.where(col_ids <= row_ids, scores, -1e30)
    highest = lax.stop_gradient(jnp.max(scores, -1, keepdims=True))
    exponent = jnp.exp(scores - highest)
    weights = (exponent / jnp.sum(exponent, -1, keepdims=True)).astype(jnp.bfloat16)
    context = jnp.einsum(
        "grqk,kgd->qgrd", weights.astype(jnp.float32), value_heads.astype(jnp.float32)
    )
    context = context.astype(jnp.bfloat16).reshape(length, query_count * HEAD_DIM)
    return lax.dot_general(
        context, output_matrix, (((1,), (1,)), ((), ())), preferred_element_type=jnp.float32
    )


def server_pull(rows_in, upstream_rows, gain, gate_matrix, up_matrix, down_matrix):
    rows_float = rows_in.astype(jnp.float32)
    inv_rms = lax.rsqrt(jnp.mean(rows_float * rows_float, -1, keepdims=True) + 1e-05)
    gain_float = gain.astype(jnp.float32)
    server_normed = (rows_float * inv_rms * gain_float).astype(jnp.bfloat16)
    gate_value = jnp.dot(server_normed, gate_matrix, preferred_element_type=jnp.float32)
    up_value = jnp.dot(server_normed, up_matrix, preferred_element_type=jnp.float32)
    pulled = lax.dot_general(
        upstream_rows, down_matrix, (((1,), (1,)), ((), ())), preferred_element_type=jnp.float32
    )
    sigmoid_gate = jax.nn.sigmoid(gate_value)
    gate_grad = (
        pulled * up_value * sigmoid_gate * (1.0 + gate_value * (1.0 - sigmoid_gate))
    ).astype(jnp.bfloat16)
    up_grad = (pulled * gate_value * sigmoid_gate).astype(jnp.bfloat16)
    normed_grad = lax.dot_general(
        gate_grad, gate_matrix, (((1,), (1,)), ((), ())), preferred_element_type=jnp.float32
    )
    normed_grad = normed_grad + lax.dot_general(
        up_grad, up_matrix, (((1,), (1,)), ((), ())), preferred_element_type=jnp.float32
    )
    weighted = normed_grad * gain_float
    return inv_rms * weighted - rows_float * inv_rms**3 * jnp.mean(
        weighted * rows_float, -1, keepdims=True
    )


def over_clients(pieces):
    return lax.all_to_all(pieces, "client", split_axis=1, concat_axis=1, tiled=True)


def over_groups(pieces):
    return lax.all_to_all(pieces, "sdata", split_axis=1, concat_axis=1, tiled=True)


def relay_out(stacked, group_order, client_count):
    count_rows, length, breadth = stacked.shape
    pieces = stacked.reshape(count_rows, client_count, length // client_count, breadth)
    arrived = jnp.take(over_clients(pieces), group_order, axis=1)
    return over_groups(arrived).reshape(count_rows, length, breadth)


def relay_back(stacked, inverse, client_count):
    count_rows, length, breadth = stacked.shape
    pieces = stacked.reshape(count_rows, client_count, length // client_count, breadth)
    arrived = jnp.take(over_groups(pieces), inverse, axis=1)
    return over_clients(arrived).reshape(count_rows, length, breadth)


def share_sum(partial_rows):
    return sum_at_owner(partial_rows.astype(jnp.bfloat16), "tensor", 1)


def widen_rows(stacked):
    return lax.all_gather(stacked, "tensor", axis=2, tiled=True)


def local(
    client_input,
    client_gain,
    query_weight,
    key_weight,
    client_value_weight,
    output_weight,
    server_gain,
    server_gate,
    server_up,
    server_down,
    upstream,
    assignment,
):
    client_count = lax.axis_size("client")
    normed = normalize(client_input, client_gain[0])
    attended, pullback = jax.vjp(
        partial(attention_part, normed),
        query_weight[0],
        key_weight[0],
        client_value_weight[0],
        output_weight[0],
    )
    group_order = jnp.argsort(assignment, stable=True)
    inverse = jnp.argsort(group_order, stable=True)
    shard_width = client_input.shape[1] // lax.axis_size("tensor")
    shard_start = lax.axis_index("tensor") * shard_width
    own_input = lax.dynamic_slice_in_dim(client_input, shard_start, shard_width, 1)
    own_upstream = lax.dynamic_slice_in_dim(upstream, shard_start, shard_width, 1)
    cut_input = (own_input.astype(jnp.float32) + share_sum(attended)).astype(jnp.bfloat16)
    arrived = relay_out(jnp.stack([cut_input, own_upstream]), group_order, client_count)
    widened = widen_rows(arrived)
    pulled = server_pull(
        widened[0], widened[1], server_gain[0], server_gate[0], server_up[0], server_down[0]
    )
    cut_grad = (share_sum(pulled) + arrived[1].astype(jnp.float32)).astype(jnp.bfloat16)
    returned = relay_back(cut_grad[None], inverse, client_count)
    arriving_grad = widen_rows(returned)[0]
    query_grad, key_grad, value_grad, output_grad = pullback(arriving_grad.astype(jnp.float32))
    query_width = query_grad.shape[1]
    key_width = key_grad.shape[1]
    joined_grads = jnp.concatenate(
        [
            query_grad.astype(jnp.float32),
            key_grad.astype(jnp.float32),
            value_grad.astype(jnp.float32),
            output_grad.astype(jnp.float32),
        ],
        1,
    )
    summed = sum_at_owner(joined_grads.astype(jnp.bfloat16), ("client", "sdata"), 0) / client_count
    query_update = summed[:, :query_width].astype(jnp.bfloat16)
    key_update = summed[:, query_width : query_width + key_width].astype(jnp.bfloat16)
    value_update = summed[:, query_width + key_width : query_width + 2 * key_width].astype(
        jnp.bfloat16
    )
    output_update = summed[:, query_width + 2 * key_width :].astype(jnp.bfloat16)
    return (query_update, key_update, value_update, output_update)


def solution(mesh):
    placed = (
        P(("client", "sdata"), None),
        P("client", None),
        P("client", None, "tensor"),
        P("client", None, "tensor"),
        P("client", None, "tensor"),
        P("client", None, "tensor"),
        P("sdata", None),
        P("sdata", None, "tensor"),
        P("sdata", None, "tensor"),
        P("sdata", "tensor", None),
        P(("client", "sdata"), None),
        P(),
    )
    return jax.shard_map(
        local,
        mesh=mesh,
        in_specs=placed,
        out_specs=(
            P(("client", "sdata"), "tensor"),
            P(("client", "sdata"), "tensor"),
            P(("client", "sdata"), "tensor"),
            P(("client", "sdata"), "tensor"),
        ),
        check_vma=False,
    )
```

profile of v0, /device:TPU:4, one launch (start us, length us, event | category | flops | bytes accessed | tf_op | source)
XLA Modules:
  0.0 317.1 jit_solution(7294213297382398546)
XLA Ops:
  7.3 0.8 mul.298
  8.1 1.9 fusion.3
  10.0 2.1 fusion.91
  12.2 1.4 copy.27
  13.6 2.6 fusion.36
  16.3 0.7 fusion.74
  17.9 0.7 copy-done.14
  18.6 0.6 fusion.31
  19.8 0.8 fusion.54
  20.7 0.6 copy-done.5
  21.3 0.6 convolution_convert_fusion
  21.9 1.2 copy.46
  23.1 6.4 %all-to-all-start = ((bf16[8,384,256]{2,1,0:T(8,128)(2,1)}), bf16[8,384,256]{2,1,0:T(8,128)(2,1)}, u32[]{:S(2)}, u32[]{:S(2)}) async-start(bf16[8,384,256]{2,1,0:T(8,128)(2,1)} %bitcast.249), calls=%async_computation | async-start | bytes 3145728 | tf_op jit(solution)/shard_map/all_to_all | solution.py:18
  29.6 1.0 constant_dynamic-slice_fusion
  30.5 17.5 %all-to-all-done = bf16[8,384,256]{2,1,0:T(8,128)(2,1)} async-done(((bf16[8,384,256]{2,1,0:T(8,128)(2,1)}), bf16[8,384,256]{2,1,0:T(8,128)(2,1)}, u32[]{:S(2)}, u32[]{:S(2)}) %all-to-all-start) | async-done | bytes 1572896 | tf_op jit(solution)/shard_map/all_to_all | solution.py:18
  48.1 1.7 convert_reduce_fusion.2
  49.7 1.0 add_convert_fusion.1
  50.7 0.8 pad_maximum_fusion.1
  51.5 8.0 %all-to-all-start.1 = ((bf16[2,16,24,256]{3,2,0,1:T(8,128)(2,1)}), bf16[2,16,24,256]{3,2,0,1:T(8,128)(2,1)S(1)}, u32[]{:S(2)}, u32[]{:S(2)}) async-start(bf16[2,16,24,256]{3,2,0,1:T(8,128)(2,1)} %pad_maximum_fusion.1), calls=%async_computation.1 | async-start | bytes 786432 | tf_op jit(solution)/shard_map/all_to_all | solution.py:114
  59.6 1.3 sort.31
  60.9 0.6 compare_select_fusion
  61.5 0.6 compare_and_fusion
  62.1 10.1 %all-to-all-done.1 = bf16[2,16,24,256]{3,2,0,1:T(8,128)(2,1)S(1)} async-done(((bf16[2,16,24,256]{3,2,0,1:T(8,128)(2,1)}), bf16[2,16,24,256]{3,2,0,1:T(8,128)(2,1)S(1)}, u32[]{:S(2)}, u32[]{:S(2)}) %all-to-all-start.1) | async-done | bytes 393248 | tf_op jit(solution)/shard_map/all_to_all | solution.py:114
  72.2 0.8 copy.30
  73.0 1.6 gather_fusion
  74.6 11.3 %all_to_all.35 = bf16[2,16,24,256]{3,2,0,1:T(8,128)(2,1)S(1)} all-to-all(bf16[2,16,24,256]{3,2,0,1:T(8,128)(2,1)S(1)} %select_bitcast_fusion), channel_id=1, replica_groups=mesh['client'=16,'tensor'=8,'sdata'=2] {'sdata'}, dimensions={1} | all-to-all | bytes 786432 | tf_op jit(solution)/shard_map/all_to_all | solution.py:118
  86.0 0.8 copy.31
  86.8 0.7 mul.299
  87.5 29.4 %all-gather.3.cloned.1.call-done = bf16[2,384,2048]{2,1,0:T(8,128)(2,1)} async-done(((bf16[2,384,256]{2,1,0:T(8,128)(2,1)}), bf16[2,384,2048]{2,1,0:T(8,128)(2,1)}) %all-gather.3.cloned.1.call-update) | async-done | bytes 3145744 | tf_op jit(solution)/shard_map/all_gather | solution.py:140
  116.9 1.8 fusion.6
  118.7 0.6 multiply_multiply_fusion
  119.3 4.1 %fusion.29 = f32[384,512]{1,0:T(8,128)} fusion(bf16[1,512,2048]{2,1,0:T(8,128)(2,1)} %param.21, bf16[2,384,2048]{2,1,0:T(8,128)(2,1)} %all-gather.3.cloned.1.call-done), kind=kOutput, calls=%fused_computation.50 | convolution fusion | flops 805306368 | bytes 4456448 | tf_op jit(solution)/shard_map/dot_general | solution.py:93
  123.5 1.9 fusion.24
  125.4 6.3 %fusion.22 = f32[384,2048]{1,0:T(8,128)} fusion(bf16[1,2048,512]{2,1,0:T(8,128)(2,1)} %param.19, f32[384,512]{1,0:T(8,128)} %fusion.29, bf16[1,2048,512]{2,1,0:T(8,128)(2,1)S(1)} %copy-done, f32[384,512]{1,0:T(8,128)} %fusion.24, f32[2048]{0:T(1024)S(1)} %bitcast.271, f32[384]{0:T(512)} %copy-done.29, bf16[2,384,2048]{2,1,0:T(8,128)(2,1)} %all-gather.3.cloned.1.call-done), kind=kOutput, calls=%fused_computation.43 | convolution fusion | flops 1615724544 | bytes 10496000 | tf_op jit(solution)/shard_map/dot_general | solution.py:101
  131.7 4.2 %fusion.10 = (f32[384]{0:T(512)S(1)}, f32[384,2048]{1,0:T(8,128)S(1)}) fusion(bf16[2,384,2048]{2,1,0:T(8,128)(2,1)} %all-gather.3.cloned.1.call-done, f32[2048]{0:T(1024)S(1)} %bitcast.272, f32[384,2048]{1,0:T(8,128)} %fusion.22, bf16[1,2048,512]{2,1,0:T(8,128)(2,1)S(1)} %copy-done, f32[384,512]{1,0:T(8,128)} %fusion.29, f32[384,512]{1,0:T(8,128)} %fusion.24), kind=kOutput, calls=%fused_computation.17 | convolution fusion | flops 810417792 | bytes 11544064 | tf_op jit(solution)/shard_map/dot_general | solution.py:104
  135.9 0.6 fusion.9
  136.5 1.2 copy.45
  137.8 5.0 %all-to-all-start.3 = ((bf16[8,384,256]{2,1,0:T(8,128)(2,1)}), bf16[8,384,256]{2,1,0:T(8,128)(2,1)}, u32[]{:S(2)}, u32[]{:S(2)}) async-start(bf16[8,384,256]{2,1,0:T(8,128)(2,1)} %bitcast.250), calls=%async_computation.3 | async-start | bytes 3145728 | tf_op jit(solution)/shard_map/all_to_all | solution.py:18
  143.3 1.9 sort.32
  145.2 1.2 compare_select_fusion.1
  146.4 1.2 compare_and_fusion.1
  147.5 13.8 %all-to-all-done.3 = bf16[8,384,256]{2,1,0:T(8,128)(2,1)} async-done(((bf16[8,384,256]{2,1,0:T(8,128)(2,1)}), bf16[8,384,256]{2,1,0:T(8,128)(2,1)}, u32[]{:S(2)}, u32[]{:S(2)}) %all-to-all-start.3) | async-done | bytes 1572896 | tf_op jit(solution)/shard_map/all_to_all | solution.py:18
  161.3 1.7 convert_reduce_fusion.1
  163.0 0.7 add_convert_fusion
  163.7 4.4 %all-to-all-start.4 = ((bf16[1,16,24,256]{3,2,0,1:T(8,128)(2,1)}), bf16[1,16,24,256]{3,2,0,1:T(8,128)(2,1)S(1)}, u32[]{:S(2)}, u32[]{:S(2)}) async-start(bf16[1,16,24,256]{3,2,0,1:T(8,128)(2,1)} %add_convert_fusion), calls=%async_computation.4 | async-start | bytes 393216 | tf_op jit(solution)/shard_map/all_to_all | solution.py:118
  168.1 0.7 pad_clamp_fusion
  168.8 5.7 %all-to-all-done.4 = bf16[1,16,24,256]{3,2,0,1:T(8,128)(2,1)S(1)} async-done(((bf16[1,16,24,256]{3,2,0,1:T(8,128)(2,1)}), bf16[1,16,24,256]{3,2,0,1:T(8,128)(2,1)S(1)}, u32[]{:S(2)}, u32[]{:S(2)}) %all-to-all-start.4) | async-done | bytes 196640 | tf_op jit(solution)/shard_map/all_to_all | solution.py:118
  174.4 1.2 gather_fusion.1
  175.7 1.0 fusion.94
  176.7 15.7 %all_to_all.36 = bf16[1,16,24,256]{3,2,0,1:T(8,128)(2,1)} all-to-all(bf16[1,16,24,256]{3,2,0,1:T(8,128)(2,1)S(1)} %fusion.94), channel_id=1, replica_groups=mesh['client'=16,'tensor'=8,'sdata'=2] {'client'}, dimensions={1} | all-to-all | bytes 393216 | tf_op jit(solution)/shard_map/all_to_all | solution.py:114
  192.5 23.7 %all-gather.5.cloned.1.call-done = bf16[1,384,2048]{2,1,0:T(8,128)(2,1)} async-done(((bf16[1,384,256]{2,1,0:T(8,128)(2,1)}), bf16[1,384,2048]{2,1,0:T(8,128)(2,1)}) %all-gather.5.cloned.1.call-update) | async-done | bytes 1572880 | tf_op jit(solution)/shard_map/all_gather | solution.py:140
  216.2 2.3 fusion.57
  218.5 1.7 fusion.21
  220.3 1.1 broadcast_multiply_fusion
  221.4 1.2 fusion.68
  222.7 4.1 %convolution_convert_fusion.3 = bf16[2048,64]{0,1:T(8,128)(2,1)} fusion(bf16[64,4,384]{2,0,1:T(8,128)(2,1)S(1)} %bitcast.269, f32[4,384]{1,0:T(4,128)S(1)} %copy-done.27, f32[4,384]{1,0:T(4,128)S(1)} %get-tuple-element.27, f32[384,384,4]{1,0,2:T(8,128)} %copy-done.1, pred[384,384]{0,1:T(8,128)(4,1)S(1)} %copy-done.9, bf16[384,2048]{1,0:T(8,128)(2,1)} %param.12, ...), kind=kOutput, calls=%fused_computation.41 | convolution fusion | flops 182411264 | bytes 4560384 | tf_op jit(solution)/shard_map/transpose(jvp())/dot_general | solution.py:64
  226.9 3.4 %convolution_convert_fusion.2 = bf16[2048,256]{1,0:T(8,128)(2,1)} fusion(bf16[384,256]{0,1:T(8,128)(2,1)S(1)} %bitcast.267, bf16[384,2048]{1,0:T(8,128)(2,1)} %param.12, f32[2048]{0:T(1024)S(1)} %bitcast.277, f32[384]{0:T(512)S(1)} %copy-done.34), kind=kOutput, calls=%fused_computation.28 | convolution fusion | flops 405798912 | bytes 2827776 | tf_op jit(solution)/shard_map/transpose(jvp())/dot_general | solution.py:51
  230.4 0.6 convolution_convert_fusion.4
  231.3 1.2 copy.40
  232.5 2.2 convolution_convert_fusion.1
  234.8 1.3 pad_maximum_fusion
  236.0 72.6 %all_to_all.37 = bf16[32,64,640]{2,1,0:T(8,128)(2,1)S(1)} all-to-all(bf16[32,64,640]{2,1,0:T(8,128)(2,1)S(1)} %pad_maximum_fusion), channel_id=1, replica_groups=mesh['client'=16,'tensor'=8,'sdata'=2] {'client','sdata'}, dimensions={0} | all-to-all | bytes 5242880 | tf_op jit(solution)/shard_map/all_to_all | solution.py:18
  309.0 0.6 fusion.122
  309.6 0.7 fusion.123
  (104 shorter events, 3.2 us)
Async XLA Ops:
  7.2 118.2 %copy-start = (bf16[1,2048,512]{2,1,0:T(8,128)(2,1)S(1)}, bf16[1,2048,512]{2,1,0:T(8,128)(2,1)}, u32[]{:S(2)}) copy-start(bf16[1,2048,512]{2,1,0:T(8,128)(2,1)} %param.20) | copy-start | bytes 6291460
  7.3 12.5 %copy-start.8 = (pred[384,384]{0,1:T(8,128)(4,1)}, pred[384,384]{0,1:T(8,128)(4,1)S(1)}, u32[]{:S(2)}) copy-start(pred[384,384]{0,1:T(8,128)(4,1)S(1)} %iota_compare_fusion) | copy-start | bytes 442372
  8.1 8.2 %copy-start.31 = (f32[1,2048]{1,0:T(1,128)}, f32[1,2048]{1,0:T(1,128)S(1)}, u32[]{:S(2)}) copy-start(f32[1,2048]{1,0:T(1,128)S(1)} %mul.298) | copy-start | bytes 24580
  8.1 4.0 %copy-start.10 = (bf16[1,2048,256]{2,1,0:T(8,128)(2,1)S(1)}, bf16[1,2048,256]{2,1,0:T(8,128)(2,1)}, u32[]{:S(2)}) copy-start(bf16[1,2048,256]{2,1,0:T(8,128)(2,1)} %param.14) | copy-start | bytes 3145732
  10.0 6.2 %copy-start.33 = (f32[384]{0:T(512)}, f32[384]{0:T(512)S(1)}, u32[]{:S(2)}) copy-start(f32[384]{0:T(512)S(1)} %add_rsqrt_fusion.1) | copy-start | bytes 4612
  13.6 2.7 copy-start.6
  13.6 2.7 copy-start.36
  17.0 2.8 copy-start.38
  17.2 2.0 copy-start.18
  17.3 2.0 copy-start.22
  17.3 0.7 copy-start.12
  17.3 1.9 copy-start.20
  17.3 1.9 copy-start.24
  17.9 0.7 copy-start.14
  19.2 1.5 copy-start.1
  19.8 0.9 copy-start.26
  19.8 1.5 copy-start.5
  20.7 2.4 copy-start.16
  23.1 24.9 %all-to-all-start = ((bf16[8,384,256]{2,1,0:T(8,128)(2,1)}), bf16[8,384,256]{2,1,0:T(8,128)(2,1)}, u32[]{:S(2)}, u32[]{:S(2)}) async-start(bf16[8,384,256]{2,1,0:T(8,128)(2,1)} %bitcast.249), calls=%async_computation | async-start | bytes 3145728 | tf_op jit(solution)/shard_map/all_to_all | solution.py:18
  29.5 30.0 %copy-start.37 = (s32[16]{0:T(128)S(1)}, s32[16]{0:T(128)}, u32[]{:S(2)}) copy-start(s32[16]{0:T(128)} %param.23) | copy-start | bytes 196
  51.5 20.7 %all-to-all-start.1 = ((bf16[2,16,24,256]{3,2,0,1:T(8,128)(2,1)}), bf16[2,16,24,256]{3,2,0,1:T(8,128)(2,1)S(1)}, u32[]{:S(2)}, u32[]{:S(2)}) async-start(bf16[2,16,24,256]{3,2,0,1:T(8,128)(2,1)} %pad_maximum_fusion.1), calls=%async_computation.1 | async-start | bytes 786432 | tf_op jit(solution)/shard_map/all_to_all | solution.py:114
  59.5 57.4 %all-gather.3.cloned.1.call-start = ((), (), s32[]{:S(2)}) async-start(), calls=%async_computation.7 | async-start | bytes 3538944 | tf_op jit(solution)/shard_map/all_gather | solution.py:140
  119.3 4.2 %copy-start.29 = (f32[384]{0:T(512)}, f32[384]{0:T(512)S(1)}, u32[]{:S(2)}) copy-start(f32[384]{0:T(512)S(1)} %get-tuple-element.26) | copy-start | bytes 4612
  119.3 4.2 %copy-start.3 = (bf16[2,384,2048]{2,1,0:T(8,128)(2,1)S(1)}, bf16[2,384,2048]{2,1,0:T(8,128)(2,1)}, u32[]{:S(2)}) copy-start(bf16[2,384,2048]{2,1,0:T(8,128)(2,1)} %all-gather.3.cloned.1.call-done) | copy-start | bytes 9437188
  119.3 4.2 %copy-start.35 = (bf16[1,2048,512]{2,1,0:T(8,128)(2,1)S(1)}, bf16[1,2048,512]{2,1,0:T(8,128)(2,1)}, u32[]{:S(2)}) copy-start(bf16[1,2048,512]{2,1,0:T(8,128)(2,1)} %param.19) | copy-start | bytes 6291460
  131.6 4.2 %copy-start.4 = (bf16[2,384,2048]{2,1,0:T(8,128)(2,1)S(1)}, bf16[2,384,2048]{2,1,0:T(8,128)(2,1)}, u32[]{:S(2)}) copy-start(bf16[2,384,2048]{2,1,0:T(8,128)(2,1)} %all-gather.3.cloned.1.call-done) | copy-start | bytes 9437188
  131.6 4.2 %copy-start.28 = (f32[384]{0:T(512)S(1)}, f32[384]{0:T(512)}, u32[]{:S(2)}) copy-start(f32[384]{0:T(512)} %get-tuple-element.25) | copy-start | bytes 4612
  131.7 4.2 %copy-start.30 = (f32[384]{0:T(512)S(1)}, f32[384]{0:T(512)}, u32[]{:S(2)}) copy-start(f32[384]{0:T(512)} %copy-done.29) | copy-start | bytes 4612
  137.8 23.5 %all-to-all-start.3 = ((bf16[8,384,256]{2,1,0:T(8,128)(2,1)}), bf16[8,384,256]{2,1,0:T(8,128)(2,1)}, u32[]{:S(2)}, u32[]{:S(2)}) async-start(bf16[8,384,256]{2,1,0:T(8,128)(2,1)} %bitcast.250), calls=%async_computation.3 | async-start | bytes 3145728 | tf_op jit(solution)/shard_map/all_to_all | solution.py:18
  142.8 49.7 %copy-start.27 = (f32[4,384]{1,0:T(4,128)S(1)}, f32[4,384]{1,0:T(4,128)}, u32[]{:S(2)}) copy-start(f32[4,384]{1,0:T(4,128)} %copy-done.26) | copy-start | bytes 18436
  163.7 54.8 %copy-start.9 = (pred[384,384]{0,1:T(8,128)(4,1)S(1)}, pred[384,384]{0,1:T(8,128)(4,1)}, u32[]{:S(2)}) copy-start(pred[384,384]{0,1:T(8,128)(4,1)} %copy-done.8) | copy-start | bytes 442372
  163.7 10.7 %all-to-all-start.4 = ((bf16[1,16,24,256]{3,2,0,1:T(8,128)(2,1)}), bf16[1,16,24,256]{3,2,0,1:T(8,128)(2,1)S(1)}, u32[]{:S(2)}, u32[]{:S(2)}) async-start(bf16[1,16,24,256]{3,2,0,1:T(8,128)(2,1)} %add_convert_fusion), calls=%async_computation.4 | async-start | bytes 393216 | tf_op jit(solution)/shard_map/all_to_all | solution.py:118
  168.1 48.0 %all-gather.5.cloned.1.call-start = ((), (), s32[]{:S(2)}) async-start(), calls=%async_computation.8 | async-start | bytes 1769472 | tf_op jit(solution)/shard_map/all_gather | solution.py:140
  216.2 2.3 copy-start.2
  218.5 1.8 copy-start.21
  218.5 1.8 copy-start.25
  220.3 1.1 copy-start.15
  221.4 1.2 copy-start.32
  221.4 1.2 copy-start.34
  222.7 4.2 %copy-start.13 = (f32[384,64]{0,1:T(8,128)S(1)}, f32[384,64]{0,1:T(8,128)}, u32[]{:S(2)}) copy-start(f32[384,64]{0,1:T(8,128)} %copy-done.12) | copy-start | bytes 294916
  226.8 3.5 %copy-start.19 = (f32[384,32]{0,1:T(8,128)S(1)}, f32[384,32]{0,1:T(8,128)}, u32[]{:S(2)}) copy-start(f32[384,32]{0,1:T(8,128)} %copy-done.18) | copy-start | bytes 147460
  226.9 3.5 %copy-start.7 = (bf16[384,2048]{1,0:T(8,128)(2,1)S(1)}, bf16[384,2048]{1,0:T(8,128)(2,1)}, u32[]{:S(2)}) copy-start(bf16[384,2048]{1,0:T(8,128)(2,1)} %param.12) | copy-start | bytes 4718596
  226.9 3.5 %copy-start.23 = (f32[384,32]{0,1:T(8,128)S(1)}, f32[384,32]{0,1:T(8,128)}, u32[]{:S(2)}) copy-start(f32[384,32]{0,1:T(8,128)} %copy-done.22) | copy-start | bytes 147460
  230.3 2.2 copy-start.17
  232.5 2.3 copy-start.11
Sparse Core Ops, SparseCore 0:
  86.9 29.9 all-gather.2
  192.6 23.5 all-gather.4
where the time goes:
time: 318 us; the launch traced here: 317 us
  waiting for transfers between devices  100 us (31%)
  blocking collectives  99.6 us (31%)
  matrix products  40.7 us (13%)
  starting transfers between devices  23.9 us (8%)
  other arithmetic  23.6 us (7%)
  between operations  14.7 us (5%)
  local copies, waits for them, and re-layouts  14.5 us (5%)
    all_to_all x1, blocking collectives, sum_at_owner(): lax.all_to_all(cut_along(value, dim, length), axis, 0, 0, tiled=True)  72.6 us
    all_gather x2, waiting for transfers between devices, widen_rows(): return lax.all_gather(stacked, 'tensor', axis=2, tiled=True)  53.1 us
    all_to_all x2, waiting for transfers between devices, sum_at_owner(): lax.all_to_all(cut_along(value, dim, length), axis, 0, 0, tiled=True)  31.3 us
    all_to_all x1, blocking collectives, over_clients(): lax.all_to_all(pieces, 'client', split_axis=1, concat_axis=1, tiled=True)  15.7 us
    all_to_all x2, starting transfers between devices, sum_at_owner(): lax.all_to_all(cut_along(value, dim, length), axis, 0, 0, tiled=True)  11.4 us
    all_to_all x1, blocking collectives, over_groups(): lax.all_to_all(pieces, 'sdata', split_axis=1, concat_axis=1, tiled=True)  11.3 us
    all_to_all x1, waiting for transfers between devices, over_clients(): lax.all_to_all(pieces, 'client', split_axis=1, concat_axis=1, tiled=True)  10.1 us
    all_to_all x1, starting transfers between devices, over_clients(): lax.all_to_all(pieces, 'client', split_axis=1, concat_axis=1, tiled=True)  8.01 us
  transfers between devices with their start and end apart: 6, of which 6 were waited for; matrix products, arithmetic and copies ran while one was open for 3% of the time, Pallas kernels for 0%

commit v1 on v0

--- a/solution.py
+++ b/solution.py
@@ -6,6 +6,19 @@
 from jax.sharding import PartitionSpec as P
 
 HEAD_DIM = 64
+
+
+def collect(x, axis, dim):
+    ways = lax.axis_size(axis)
+    up = [(d, (d + 1) % ways) for d in range(ways)]
+    down = [(d, (d - 1) % ways) for d in range(ways)]
+    earlier, later = ([x], [x])
+    for _ in range(ways // 2):
+        earlier.append(lax.ppermute(earlier[-1], axis, up))
+    for _ in range((ways - 1) // 2):
+        later.append(lax.ppermute(later[-1], axis, down))
+    line = jnp.concatenate([*earlier[::-1], *later[1:]], axis=dim)
+    return jnp.roll(line, (lax.axis_index(axis) - ways // 2) * x.shape[dim], axis=dim)
 
 
 def cut_along(value, dim, length):
@@ -137,7 +150,7 @@
 
 
 def widen_rows(stacked):
-    return lax.all_gather(stacked, "tensor", axis=2, tiled=True)
+    return collect(stacked, "tensor", 2)
 
 
 def local(

time: 318 us -> 312 us (0.981)
  starting transfers between devices: 23.9 us -> 41.1 us
  waiting for transfers between devices: 100 us -> 84.1 us
  local copies, waits for them, and re-layouts: 14.5 us -> 27.8 us
  between operations: 14.7 us -> 1.65 us
  blocking collectives: 99.6 us -> 92.2 us
  matrix products: 40.7 us -> 36.9 us
    all_gather x2 -> x0, waiting for transfers between devices: 53.1 us -> none  [widen_rows(): return lax.all_gather(stacked, 'tensor', axis=2, tiled=True)]
    ppermute x0 -> x14, waiting for transfers between devices: none -> 37.6 us  [the longest x8 37.5 us: collect(): earlier.append(lax.ppermute(earlier[-1], axis, up))]
    unnamed x79 -> x125, local copies, waits for them, and re-layouts: 3.43 us -> 16.5 us
    ppermute x0 -> x14, starting transfers between devices: none -> 11.3 us  [the longest x6 11 us: collect(): later.append(lax.ppermute(later[-1], axis, down))]
    all_to_all x2, starting transfers between devices: 11.4 us -> 18.3 us  [sum_at_owner(): lax.all_to_all(cut_along(value, dim, length), axis, 0, 0, tiled=True)]
    all_to_all x1, blocking collectives: 72.6 us -> 67.9 us  [sum_at_owner(): lax.all_to_all(cut_along(value, dim, length), axis, 0, 0, tiled=True)]
  transfers between devices with their start and end apart: 6 -> 18, of which waited for: 6 -> 13; matrix products, arithmetic and copies ran while one was open for 3% -> 5% of each run, Pallas kernels for 0% -> 0%
where the time goes in v1:
time: 312 us; the launch traced here: 309 us
  blocking collectives  92.2 us (30%)
  waiting for transfers between devices  84.1 us (27%)
  starting transfers between devices  41.1 us (13%)
  matrix products  36.9 us (12%)
  local copies, waits for them, and re-layouts  27.8 us (9%)
  other arithmetic  25.6 us (8%)
    all_to_all x1, blocking collectives, sum_at_owner(): lax.all_to_all(cut_along(value, dim, length), axis, 0, 0, tiled=True)  67.9 us
    ppermute x8, waiting for transfers between devices, collect(): earlier.append(lax.ppermute(earlier[-1], axis, up))  37.5 us
    all_to_all x2, waiting for transfers between devices, sum_at_owner(): lax.all_to_all(cut_along(value, dim, length), axis, 0, 0, tiled=True)  31.2 us
    all_to_all x2, starting transfers between devices, sum_at_owner(): lax.all_to_all(cut_along(value, dim, length), axis, 0, 0, tiled=True)  18.3 us
    unnamed x125, local copies, waits for them, and re-layouts  16.5 us
    all_to_all x1, blocking collectives, over_clients(): lax.all_to_all(pieces, 'client', split_axis=1, concat_axis=1, tiled=True)  13 us
    all_to_all x1, blocking collectives, over_groups(): lax.all_to_all(pieces, 'sdata', split_axis=1, concat_axis=1, tiled=True)  11.4 us
    ppermute x6, starting transfers between devices, collect(): later.append(lax.ppermute(later[-1], axis, down))  11 us
  transfers between devices with their start and end apart: 18, of which 13 were waited for; matrix products, arithmetic and copies ran while one was open for 5% of the time, Pallas kernels for 0%

profile of v1, /device:TPU:4, one launch (start us, length us, event | category | flops | bytes accessed | tf_op | source)
XLA Modules:
  0.0 309.3 jit_solution(15963666010880031246)
XLA Ops:
  1.7 1.8 fusion.3
  3.5 2.1 fusion.93
  5.6 1.4 copy.27
  7.1 2.6 fusion.36
  14.7 1.2 copy.46
  16.0 6.4 %all-to-all-start = ((bf16[8,384,256]{2,1,0:T(8,128)(2,1)}), bf16[8,384,256]{2,1,0:T(8,128)(2,1)}, u32[]{:S(2)}, u32[]{:S(2)}) async-start(bf16[8,384,256]{2,1,0:T(8,128)(2,1)} %bitcast.249), calls=%async_computation | async-start | bytes 3145728 | tf_op jit(solution)/shard_map/all_to_all | solution.py:31
  23.3 17.5 %all-to-all-done = bf16[8,384,256]{2,1,0:T(8,128)(2,1)} async-done(((bf16[8,384,256]{2,1,0:T(8,128)(2,1)}), bf16[8,384,256]{2,1,0:T(8,128)(2,1)}, u32[]{:S(2)}, u32[]{:S(2)}) %all-to-all-start) | async-done | bytes 1572896 | tf_op jit(solution)/shard_map/all_to_all | solution.py:31
  40.9 1.7 convert_reduce_fusion.2
  44.3 8.0 %all-to-all-start.1 = ((bf16[2,16,24,256]{3,2,0,1:T(8,128)(2,1)}), bf16[2,16,24,256]{3,2,0,1:T(8,128)(2,1)S(1)}, u32[]{:S(2)}, u32[]{:S(2)}) async-start(bf16[2,16,24,256]{3,2,0,1:T(8,128)(2,1)} %pad_maximum_fusion.1), calls=%async_computation.1 | async-start | bytes 786432 | tf_op jit(solution)/shard_map/all_to_all | solution.py:127
  52.3 1.3 sort.31
  54.9 10.1 %all-to-all-done.1 = bf16[2,16,24,256]{3,2,0,1:T(8,128)(2,1)S(1)} async-done(((bf16[2,16,24,256]{3,2,0,1:T(8,128)(2,1)}), bf16[2,16,24,256]{3,2,0,1:T(8,128)(2,1)S(1)}, u32[]{:S(2)}, u32[]{:S(2)}) %all-to-all-start.1) | async-done | bytes 393248 | tf_op jit(solution)/shard_map/all_to_all | solution.py:127
  65.8 1.6 gather_fusion
  67.5 11.4 %all_to_all.35 = bf16[2,16,24,256]{3,2,0,1:T(8,128)(2,1)S(1)} all-to-all(bf16[2,16,24,256]{3,2,0,1:T(8,128)(2,1)S(1)} %select_bitcast_fusion), channel_id=1, replica_groups=mesh['client'=16,'tensor'=8,'sdata'=2] {'sdata'}, dimensions={1} | all-to-all | bytes 786432 | tf_op jit(solution)/shard_map/all_to_all | solution.py:131
  78.9 7.2 %collective-permute-done = bf16[2,384,256]{2,1,0:T(8,128)(2,1)S(1)} collective-permute-done((bf16[2,384,256]{2,1,0:T(8,128)(2,1)S(1)}, bf16[2,384,256]{2,1,0:T(8,128)(2,1)S(1)}, u32[]{:S(2)}, u32[]{:S(2)}) %collective-permute-start) | collective-permute-done | bytes 393248 | tf_op jit(solution)/shard_map/ppermute | solution.py:17
  86.1 1.7 collective-permute-start.4
  87.8 5.5 %collective-permute-done.1 = bf16[2,384,256]{2,1,0:T(8,128)(2,1)S(1)} collective-permute-done((bf16[2,384,256]{2,1,0:T(8,128)(2,1)S(1)}, bf16[2,384,256]{2,1,0:T(8,128)(2,1)S(1)}, u32[]{:S(2)}, u32[]{:S(2)}) %collective-permute-start.1) | collective-permute-done | bytes 393248 | tf_op jit(solution)/shard_map/ppermute | solution.py:17
  93.3 1.8 collective-permute-start.5
  95.1 5.5 %collective-permute-done.2 = bf16[2,384,256]{2,1,0:T(8,128)(2,1)} collective-permute-done((bf16[2,384,256]{2,1,0:T(8,128)(2,1)S(1)}, bf16[2,384,256]{2,1,0:T(8,128)(2,1)}, u32[]{:S(2)}, u32[]{:S(2)}) %collective-permute-start.2) | collective-permute-done | bytes 393248 | tf_op jit(solution)/shard_map/ppermute | solution.py:17
  101.3 1.8 collective-permute-start.6
  103.1 5.0 %collective-permute-done.3 = bf16[2,384,256]{2,1,0:T(8,128)(2,1)} collective-permute-done((bf16[2,384,256]{2,1,0:T(8,128)(2,1)}, bf16[2,384,256]{2,1,0:T(8,128)(2,1)}, u32[]{:S(2)}, u32[]{:S(2)}) %collective-permute-start.3) | collective-permute-done | bytes 393248 | tf_op jit(solution)/shard_map/ppermute | solution.py:17
  108.1 1.0 constant_dynamic-update-slice_fusion.15
  109.1 1.0 constant_dynamic-update-slice_fusion.14
  110.2 1.1 constant_dynamic-update-slice_fusion.13
  111.3 1.1 constant_dynamic-update-slice_fusion.12
  112.5 1.0 constant_dynamic-update-slice_fusion.10
  113.5 1.0 constant_dynamic-update-slice_fusion.9
  114.7 1.0 constant_dynamic-update-slice_fusion.7
  115.7 1.0 constant_dynamic-update-slice_fusion.6
  116.9 1.2 constant_dynamic-update-slice_fusion.2
  118.1 1.0 constant_dynamic-update-slice_fusion.1
  119.7 1.9 fusion.29
  122.8 1.9 fusion.24
  124.7 6.3 %fusion.22 = f32[384,2048]{1,0:T(8,128)} fusion(bf16[1,2048,512]{2,1,0:T(8,128)(2,1)} %param.19, f32[384,512]{1,0:T(8,128)} %fusion.29, bf16[1,2048,512]{2,1,0:T(8,128)(2,1)S(1)} %copy-done, f32[384,512]{1,0:T(8,128)} %fusion.24, f32[2048]{0:T(1024)S(1)} %bitcast.277, f32[384]{0:T(512)S(1)} %get-tuple-element.26, bf16[2,384,4096]{2,1,0:T(8,128)(2,1)} %copy-done.4, ...), kind=kOutput, calls=%fused_computation.43 | convolution fusion | flops 1615724544 | bytes 10495492 | tf_op jit(solution)/shard_map/dot_general | solution.py:114
  131.0 4.1 %fusion.10 = (f32[384]{0:T(512)S(1)}, f32[384,2048]{1,0:T(8,128)S(1)}) fusion(bf16[2,384,4096]{2,1,0:T(8,128)(2,1)} %copy-done.4, s32[]{:T(128)S(6)} %select_n.62, f32[2048]{0:T(1024)S(1)} %bitcast.278, f32[384,2048]{1,0:T(8,128)} %fusion.22, bf16[1,2048,512]{2,1,0:T(8,128)(2,1)S(1)} %copy-done, f32[384,512]{1,0:T(8,128)} %fusion.29, f32[384,512]{1,0:T(8,128)} %fusion.24), kind=kOutput, calls=%fused_computation.17 | convolution fusion | flops 810417792 | bytes 11544068 | tf_op jit(solution)/shard_map/dot_general | solution.py:117
  135.1 2.0 fusion.9
  137.2 1.2 copy.45
  138.4 11.9 %all-to-all-start.3 = ((bf16[8,384,256]{2,1,0:T(8,128)(2,1)}), bf16[8,384,256]{2,1,0:T(8,128)(2,1)}, u32[]{:S(2)}, u32[]{:S(2)}) async-start(bf16[8,384,256]{2,1,0:T(8,128)(2,1)} %bitcast.250), calls=%async_computation.3 | async-start | bytes 3145728 | tf_op jit(solution)/shard_map/all_to_all | solution.py:31
  150.9 1.9 sort.32
  152.8 1.2 compare_select_fusion.1
  154.0 1.2 compare_and_fusion.1
  155.2 13.7 %all-to-all-done.3 = bf16[8,384,256]{2,1,0:T(8,128)(2,1)} async-done(((bf16[8,384,256]{2,1,0:T(8,128)(2,1)}), bf16[8,384,256]{2,1,0:T(8,128)(2,1)}, u32[]{:S(2)}, u32[]{:S(2)}) %all-to-all-start.3) | async-done | bytes 1572896 | tf_op jit(solution)/shard_map/all_to_all | solution.py:31
  168.9 1.7 convert_reduce_fusion.1
  171.3 3.4 %all-to-all-start.4 = ((bf16[1,16,24,256]{3,2,0,1:T(8,128)(2,1)}), bf16[1,16,24,256]{3,2,0,1:T(8,128)(2,1)S(1)}, u32[]{:S(2)}, u32[]{:S(2)}) async-start(bf16[1,16,24,256]{3,2,0,1:T(8,128)(2,1)} %add_convert_fusion), calls=%async_computation.4 | async-start | bytes 393216 | tf_op jit(solution)/shard_map/all_to_all | solution.py:131
  174.7 1.2 pad_clamp_fusion
  175.9 5.1 %all-to-all-done.4 = bf16[1,16,24,256]{3,2,0,1:T(8,128)(2,1)S(1)} async-done(((bf16[1,16,24,256]{3,2,0,1:T(8,128)(2,1)}), bf16[1,16,24,256]{3,2,0,1:T(8,128)(2,1)S(1)}, u32[]{:S(2)}, u32[]{:S(2)}) %all-to-all-start.4) | async-done | bytes 196640 | tf_op jit(solution)/shard_map/all_to_all | solution.py:131
  182.4 13.0 %all_to_all.36 = bf16[1,16,24,256]{3,2,0,1:T(8,128)(2,1)S(1)} all-to-all(bf16[1,16,24,256]{3,2,0,1:T(8,128)(2,1)S(1)} %fusion.96), channel_id=1, replica_groups=mesh['client'=16,'tensor'=8,'sdata'=2] {'client'}, dimensions={1} | all-to-all | bytes 393216 | tf_op jit(solution)/shard_map/all_to_all | solution.py:127
  195.4 5.1 %collective-permute-done.7 = bf16[1,384,256]{2,1,0:T(8,128)(2,1)S(1)} collective-permute-done((bf16[1,384,256]{2,1,0:T(8,128)(2,1)S(1)}, bf16[1,384,256]{2,1,0:T(8,128)(2,1)S(1)}, u32[]{:S(2)}, u32[]{:S(2)}) %collective-permute-start.7) | collective-permute-done | bytes 196640 | tf_op jit(solution)/shard_map/ppermute | solution.py:17
  200.6 1.6 collective-permute-start.11
  202.2 3.3 %collective-permute-done.8 = bf16[1,384,256]{2,1,0:T(8,128)(2,1)S(1)} collective-permute-done((bf16[1,384,256]{2,1,0:T(8,128)(2,1)S(1)}, bf16[1,384,256]{2,1,0:T(8,128)(2,1)S(1)}, u32[]{:S(2)}, u32[]{:S(2)}) %collective-permute-start.8) | collective-permute-done | bytes 196640 | tf_op jit(solution)/shard_map/ppermute | solution.py:17
  205.7 1.9 collective-permute-start.12
  207.6 3.1 collective-permute-done.9
  210.8 2.1 collective-permute-start.13
  212.9 2.9 collective-permute-done.10
  217.1 1.3 copy-done.2
  219.4 2.0 broadcast_multiply_fusion
  221.5 1.8 fusion.70
  223.3 4.2 %convolution_convert_fusion.3 = bf16[2048,64]{0,1:T(8,128)(2,1)} fusion(bf16[64,4,384]{2,0,1:T(8,128)(2,1)} %bitcast.274, f32[4,384]{1,0:T(4,128)S(1)} %copy-done.36, f32[4,384]{1,0:T(4,128)S(1)} %get-tuple-element.27, f32[384,384,4]{1,0,2:T(8,128)} %copy-done.1, pred[384,384]{0,1:T(8,128)(4,1)S(1)} %copy-done.15, bf16[384,2048]{1,0:T(8,128)(2,1)} %param.12, ...), kind=kOutput, calls=%fused_computation.41 | convolution fusion | flops 182411264 | bytes 4560384 | tf_op jit(solution)/shard_map/transpose(jvp())/dot_general | solution.py:77
  227.5 2.3 convolution_convert_fusion.1
  229.8 1.1 fusion.128
  231.0 1.9 convolution_convert_fusion.2
  233.0 1.3 convolution_convert_fusion.4
  234.3 2.0 copy.39
  237.3 2.4 pad_maximum_fusion
  239.7 67.9 %all_to_all.37 = bf16[32,64,640]{2,1,0:T(8,128)(2,1)S(1)} all-to-all(bf16[32,64,640]{2,1,0:T(8,128)(2,1)S(1)} %pad_maximum_fusion), channel_id=1, replica_groups=mesh['client'=16,'tensor'=8,'sdata'=2] {'client','sdata'}, dimensions={0} | all-to-all | bytes 5242880 | tf_op jit(solution)/shard_map/all_to_all | solution.py:31
  (174 shorter events, 21.4 us)
Async XLA Ops:
  0.6 124.1 %copy-start = (bf16[1,2048,512]{2,1,0:T(8,128)(2,1)S(1)}, bf16[1,2048,512]{2,1,0:T(8,128)(2,1)}, u32[]{:S(2)}) copy-start(bf16[1,2048,512]{2,1,0:T(8,128)(2,1)} %param.20) | copy-start | bytes 6291460
  0.6 5.0 %copy-start.16 = (bf16[1,2048,256]{2,1,0:T(8,128)(2,1)S(1)}, bf16[1,2048,256]{2,1,0:T(8,128)(2,1)}, u32[]{:S(2)}) copy-start(bf16[1,2048,256]{2,1,0:T(8,128)(2,1)} %param.14) | copy-start | bytes 3145732
  0.7 11.9 %copy-start.14 = (pred[384,384]{0,1:T(8,128)(4,1)}, pred[384,384]{0,1:T(8,128)(4,1)S(1)}, u32[]{:S(2)}) copy-start(pred[384,384]{0,1:T(8,128)(4,1)S(1)} %iota_compare_fusion) | copy-start | bytes 442372
  1.7 8.1 %copy-start.37 = (f32[1,2048]{1,0:T(1,128)}, f32[1,2048]{1,0:T(1,128)S(1)}, u32[]{:S(2)}) copy-start(f32[1,2048]{1,0:T(1,128)S(1)} %mul.303) | copy-start | bytes 24580
  3.5 6.3 %copy-start.39 = (f32[384]{0:T(512)}, f32[384]{0:T(512)S(1)}, u32[]{:S(2)}) copy-start(f32[384]{0:T(512)S(1)} %add_rsqrt_fusion.1) | copy-start | bytes 4612
  7.1 2.7 copy-start.8
  7.1 2.7 copy-start.43
  10.5 2.1 copy-start.45
  10.7 1.3 copy-start.23
  10.8 0.6 copy-start.32
  10.8 1.2 copy-start.17
  10.8 1.2 copy-start.26
  11.4 0.7 copy-start.19
  12.0 1.5 copy-start.1
  12.6 0.9 copy-start.35
  12.6 1.4 copy-start.3
  13.5 2.5 copy-start.21
  16.0 24.9 %all-to-all-start = ((bf16[8,384,256]{2,1,0:T(8,128)(2,1)}), bf16[8,384,256]{2,1,0:T(8,128)(2,1)}, u32[]{:S(2)}, u32[]{:S(2)}) async-start(bf16[8,384,256]{2,1,0:T(8,128)(2,1)} %bitcast.249), calls=%async_computation | async-start | bytes 3145728 | tf_op jit(solution)/shard_map/all_to_all | solution.py:31
  22.4 30.0 %copy-start.44 = (s32[16]{0:T(128)S(1)}, s32[16]{0:T(128)}, u32[]{:S(2)}) copy-start(s32[16]{0:T(128)} %param.23) | copy-start | bytes 196
  44.3 20.7 %all-to-all-start.1 = ((bf16[2,16,24,256]{3,2,0,1:T(8,128)(2,1)}), bf16[2,16,24,256]{3,2,0,1:T(8,128)(2,1)S(1)}, u32[]{:S(2)}, u32[]{:S(2)}) async-start(bf16[2,16,24,256]{3,2,0,1:T(8,128)(2,1)} %pad_maximum_fusion.1), calls=%async_computation.1 | async-start | bytes 786432 | tf_op jit(solution)/shard_map/all_to_all | solution.py:127
  78.8 14.5 %copy-start.6 = (bf16[2,16,24,256]{3,2,0,1:T(8,128)(2,1)}, bf16[2,16,24,256]{3,2,0,1:T(8,128)(2,1)S(1)}, u32[]{:S(2)}) copy-start(bf16[2,16,24,256]{3,2,0,1:T(8,128)(2,1)S(1)} %all_to_all.35) | copy-start | bytes 1179652
  78.8 7.2 %collective-permute-start = (bf16[2,384,256]{2,1,0:T(8,128)(2,1)S(1)}, bf16[2,384,256]{2,1,0:T(8,128)(2,1)S(1)}, u32[]{:S(2)}, u32[]{:S(2)}) collective-permute-start(bf16[2,384,256]{2,1,0:T(8,128)(2,1)S(1)} %bitcast.254), channel_id=1, source_target_pairs={{0,2},{2,4},{4,6},{6,8},{8,10},{10,12},{12,14},{14,0},{1,3},{3,5},... | collective-permute-start | bytes 1179656 | tf_op jit(solution)/shard_map/ppermute | solution.py:17
  86.1 9.1 %copy-start.10 = (bf16[2,384,256]{2,1,0:T(8,128)(2,1)}, bf16[2,384,256]{2,1,0:T(8,128)(2,1)S(1)}, u32[]{:S(2)}) copy-start(bf16[2,384,256]{2,1,0:T(8,128)(2,1)S(1)} %collective-permute-done) | copy-start | bytes 1179652
  86.1 7.2 %collective-permute-start.1 = (bf16[2,384,256]{2,1,0:T(8,128)(2,1)S(1)}, bf16[2,384,256]{2,1,0:T(8,128)(2,1)S(1)}, u32[]{:S(2)}, u32[]{:S(2)}) collective-permute-start(bf16[2,384,256]{2,1,0:T(8,128)(2,1)S(1)} %collective-permute-done), channel_id=1, source_target_pairs={{0,2},{2,4},{4,6},{6,8},{8,10},{10,12},{12,14},{14,0},{1,3},{3,5},... | collective-permute-start | bytes 1179656 | tf_op jit(solution)/shard_map/ppermute | solution.py:17
  86.1 7.2 %collective-permute-start.4 = (bf16[2,384,256]{2,1,0:T(8,128)(2,1)S(1)}, bf16[2,384,256]{2,1,0:T(8,128)(2,1)}, u32[]{:S(2)}, u32[]{:S(2)}) collective-permute-start(bf16[2,384,256]{2,1,0:T(8,128)(2,1)S(1)} %bitcast.255), channel_id=1, source_target_pairs={{0,14},{2,0},{4,2},{6,4},{8,6},{10,8},{12,10},{14,12},{1,15},{3,1}... | collective-permute-start | bytes 1179656 | tf_op jit(solution)/shard_map/ppermute | solution.py:19
  93.3 7.3 %copy-start.12 = (bf16[2,384,256]{2,1,0:T(8,128)(2,1)}, bf16[2,384,256]{2,1,0:T(8,128)(2,1)S(1)}, u32[]{:S(2)}) copy-start(bf16[2,384,256]{2,1,0:T(8,128)(2,1)S(1)} %collective-permute-done.1) | copy-start | bytes 1179652
  93.3 7.3 %collective-permute-start.2 = (bf16[2,384,256]{2,1,0:T(8,128)(2,1)S(1)}, bf16[2,384,256]{2,1,0:T(8,128)(2,1)}, u32[]{:S(2)}, u32[]{:S(2)}) collective-permute-start(bf16[2,384,256]{2,1,0:T(8,128)(2,1)S(1)} %collective-permute-done.1), channel_id=1, source_target_pairs={{0,2},{2,4},{4,6},{6,8},{8,10},{10,12},{12,14},{14,0},{1,3},{3,5},... | collective-permute-start | bytes 1179656 | tf_op jit(solution)/shard_map/ppermute | solution.py:17
  93.3 8.0 %collective-permute-start.5 = (bf16[2,384,256]{2,1,0:T(8,128)(2,1)}, bf16[2,384,256]{2,1,0:T(8,128)(2,1)}, u32[]{:S(2)}, u32[]{:S(2)}) collective-permute-start(bf16[2,384,256]{2,1,0:T(8,128)(2,1)} %collective-permute-done.4), channel_id=1, source_target_pairs={{0,14},{2,0},{4,2},{6,4},{8,6},{10,8},{12,10},{14,12},{1,15},{3,1}... | collective-permute-start | bytes 1179656 | tf_op jit(solution)/shard_map/ppermute | solution.py:19
  100.6 7.5 %collective-permute-start.3 = (bf16[2,384,256]{2,1,0:T(8,128)(2,1)}, bf16[2,384,256]{2,1,0:T(8,128)(2,1)}, u32[]{:S(2)}, u32[]{:S(2)}) collective-permute-start(bf16[2,384,256]{2,1,0:T(8,128)(2,1)} %collective-permute-done.2), channel_id=1, source_target_pairs={{0,2},{2,4},{4,6},{6,8},{8,10},{10,12},{12,14},{14,0},{1,3},{3,5},... | collective-permute-start | bytes 1179656 | tf_op jit(solution)/shard_map/ppermute | solution.py:17
  101.3 13.3 %collective-permute-start.6 = (bf16[2,384,256]{2,1,0:T(8,128)(2,1)}, bf16[2,384,256]{2,1,0:T(8,128)(2,1)S(1)}, u32[]{:S(2)}, u32[]{:S(2)}) collective-permute-start(bf16[2,384,256]{2,1,0:T(8,128)(2,1)} %collective-permute-done.5), channel_id=1, source_target_pairs={{0,14},{2,0},{4,2},{6,4},{8,6},{10,8},{12,10},{14,12},{1,15},{3,1}... | collective-permute-start | bytes 1179656 | tf_op jit(solution)/shard_map/ppermute | solution.py:19
  110.2 6.6 %copy-start.13 = (bf16[2,384,256]{2,1,0:T(8,128)(2,1)S(1)}, bf16[2,384,256]{2,1,0:T(8,128)(2,1)}, u32[]{:S(2)}) copy-start(bf16[2,384,256]{2,1,0:T(8,128)(2,1)} %copy-done.12) | copy-start | bytes 1179652
  111.3 5.5 %copy-start.11 = (bf16[2,384,256]{2,1,0:T(8,128)(2,1)S(1)}, bf16[2,384,256]{2,1,0:T(8,128)(2,1)}, u32[]{:S(2)}) copy-start(bf16[2,384,256]{2,1,0:T(8,128)(2,1)} %copy-done.10) | copy-start | bytes 1179652
  116.8 2.9 copy-start.41
  119.2 3.1 %copy-start.4 = (bf16[2,384,4096]{2,1,0:T(8,128)(2,1)}, bf16[2,384,4096]{2,1,0:T(8,128)(2,1)S(1)}, u32[]{:S(2)}) copy-start(bf16[2,384,4096]{2,1,0:T(8,128)(2,1)S(1)} %constant_dynamic-update-slice_fusion) | copy-start | bytes 18874372
  119.6 3.2 %copy-start.42 = (bf16[1,2048,512]{2,1,0:T(8,128)(2,1)S(1)}, bf16[1,2048,512]{2,1,0:T(8,128)(2,1)}, u32[]{:S(2)}) copy-start(bf16[1,2048,512]{2,1,0:T(8,128)(2,1)} %param.19) | copy-start | bytes 6291460
  138.4 32.1 %copy-start.7 = (bf16[2,16,24,256]{3,2,0,1:T(8,128)(2,1)S(1)}, bf16[2,16,24,256]{3,2,0,1:T(8,128)(2,1)}, u32[]{:S(2)}) copy-start(bf16[2,16,24,256]{3,2,0,1:T(8,128)(2,1)} %copy-done.6) | copy-start | bytes 1179652
  138.4 72.4 %copy-start.36 = (f32[4,384]{1,0:T(4,128)S(1)}, f32[4,384]{1,0:T(4,128)}, u32[]{:S(2)}) copy-start(f32[4,384]{1,0:T(4,128)} %copy-done.35) | copy-start | bytes 18436
  138.4 30.4 %all-to-all-start.3 = ((bf16[8,384,256]{2,1,0:T(8,128)(2,1)}), bf16[8,384,256]{2,1,0:T(8,128)(2,1)}, u32[]{:S(2)}, u32[]{:S(2)}) async-start(bf16[8,384,256]{2,1,0:T(8,128)(2,1)} %bitcast.250), calls=%async_computation.3 | async-start | bytes 3145728 | tf_op jit(solution)/shard_map/all_to_all | solution.py:31
  171.3 9.8 %all-to-all-start.4 = ((bf16[1,16,24,256]{3,2,0,1:T(8,128)(2,1)}), bf16[1,16,24,256]{3,2,0,1:T(8,128)(2,1)S(1)}, u32[]{:S(2)}, u32[]{:S(2)}) async-start(bf16[1,16,24,256]{3,2,0,1:T(8,128)(2,1)} %add_convert_fusion), calls=%async_computation.4 | async-start | bytes 393216 | tf_op jit(solution)/shard_map/all_to_all | solution.py:131
  195.4 5.1 %collective-permute-start.7 = (bf16[1,384,256]{2,1,0:T(8,128)(2,1)S(1)}, bf16[1,384,256]{2,1,0:T(8,128)(2,1)S(1)}, u32[]{:S(2)}, u32[]{:S(2)}) collective-permute-start(bf16[1,384,256]{2,1,0:T(8,128)(2,1)S(1)} %bitcast.260), channel_id=1, source_target_pairs={{0,2},{2,4},{4,6},{6,8},{8,10},{10,12},{12,14},{14,0},{1,3},{3,5},... | collective-permute-start | bytes 589832 | tf_op jit(solution)/shard_map/ppermute | solution.py:17
  200.5 5.1 %collective-permute-start.8 = (bf16[1,384,256]{2,1,0:T(8,128)(2,1)S(1)}, bf16[1,384,256]{2,1,0:T(8,128)(2,1)S(1)}, u32[]{:S(2)}, u32[]{:S(2)}) collective-permute-start(bf16[1,384,256]{2,1,0:T(8,128)(2,1)S(1)} %collective-permute-done.7), channel_id=1, source_target_pairs={{0,2},{2,4},{4,6},{6,8},{8,10},{10,12},{12,14},{14,0},{1,3},{3,5},... | collective-permute-start | bytes 589832 | tf_op jit(solution)/shard_map/ppermute | solution.py:17
  200.6 5.1 %collective-permute-start.11 = (bf16[1,384,256]{2,1,0:T(8,128)(2,1)S(1)}, bf16[1,384,256]{2,1,0:T(8,128)(2,1)S(1)}, u32[]{:S(2)}, u32[]{:S(2)}) collective-permute-start(bf16[1,384,256]{2,1,0:T(8,128)(2,1)S(1)} %bitcast.261), channel_id=1, source_target_pairs={{0,14},{2,0},{4,2},{6,4},{8,6},{10,8},{12,10},{14,12},{1,15},{3,1}... | collective-permute-start | bytes 589832 | tf_op jit(solution)/shard_map/ppermute | solution.py:19
  205.6 5.1 %collective-permute-start.9 = (bf16[1,384,256]{2,1,0:T(8,128)(2,1)S(1)}, bf16[1,384,256]{2,1,0:T(8,128)(2,1)S(1)}, u32[]{:S(2)}, u32[]{:S(2)}) collective-permute-start(bf16[1,384,256]{2,1,0:T(8,128)(2,1)S(1)} %collective-permute-done.8), channel_id=1, source_target_pairs={{0,2},{2,4},{4,6},{6,8},{8,10},{10,12},{12,14},{14,0},{1,3},{3,5},... | collective-permute-start | bytes 589832 | tf_op jit(solution)/shard_map/ppermute | solution.py:17
  205.7 5.1 %collective-permute-start.12 = (bf16[1,384,256]{2,1,0:T(8,128)(2,1)S(1)}, bf16[1,384,256]{2,1,0:T(8,128)(2,1)S(1)}, u32[]{:S(2)}, u32[]{:S(2)}) collective-permute-start(bf16[1,384,256]{2,1,0:T(8,128)(2,1)S(1)} %collective-permute-done.11), channel_id=1, source_target_pairs={{0,14},{2,0},{4,2},{6,4},{8,6},{10,8},{12,10},{14,12},{1,15},{3,1}... | collective-permute-start | bytes 589832 | tf_op jit(solution)/shard_map/ppermute | solution.py:19
  210.7 5.1 %collective-permute-start.10 = (bf16[1,384,256]{2,1,0:T(8,128)(2,1)S(1)}, bf16[1,384,256]{2,1,0:T(8,128)(2,1)S(1)}, u32[]{:S(2)}, u32[]{:S(2)}) collective-permute-start(bf16[1,384,256]{2,1,0:T(8,128)(2,1)S(1)} %collective-permute-done.9), channel_id=1, source_target_pairs={{0,2},{2,4},{4,6},{6,8},{8,10},{10,12},{12,14},{14,0},{1,3},{3,5},... | collective-permute-start | bytes 589832 | tf_op jit(solution)/shard_map/ppermute | solution.py:17
  210.8 5.3 %collective-permute-start.13 = (bf16[1,384,256]{2,1,0:T(8,128)(2,1)S(1)}, bf16[1,384,256]{2,1,0:T(8,128)(2,1)S(1)}, u32[]{:S(2)}, u32[]{:S(2)}) collective-permute-start(bf16[1,384,256]{2,1,0:T(8,128)(2,1)S(1)} %collective-permute-done.12), channel_id=1, source_target_pairs={{0,14},{2,0},{4,2},{6,4},{8,6},{10,8},{12,10},{14,12},{1,15},{3,1}... | collective-permute-start | bytes 589832 | tf_op jit(solution)/shard_map/ppermute | solution.py:19
  215.9 2.5 copy-start.2
  216.0 2.5 copy-start.15
  216.0 2.5 copy-start.46
  216.3 3.1 copy-start.5
  217.1 4.3 %copy-start.29 = (bf16[384,256]{0,1:T(8,128)(2,1)}, bf16[384,256]{0,1:T(8,128)(2,1)S(1)}, u32[]{:S(2)}) copy-start(bf16[384,256]{0,1:T(8,128)(2,1)S(1)} %fusion.60) | copy-start | bytes 589828
  217.1 2.3 copy-start.27
  217.1 2.3 copy-start.33
  219.4 2.0 copy-start.20
  221.5 1.8 copy-start.38
  221.5 1.8 copy-start.40
  223.3 4.2 %copy-start.22 = (bf16[64,4,384]{2,0,1:T(8,128)(2,1)S(1)}, bf16[64,4,384]{2,0,1:T(8,128)(2,1)}, u32[]{:S(2)}) copy-start(bf16[64,4,384]{2,0,1:T(8,128)(2,1)} %copy-done.21) | copy-start | bytes 589828
  227.5 3.5 %copy-start.18 = (f32[384,64]{0,1:T(8,128)S(1)}, f32[384,64]{0,1:T(8,128)}, u32[]{:S(2)}) copy-start(f32[384,64]{0,1:T(8,128)} %copy-done.17) | copy-start | bytes 294916
  227.5 3.5 %copy-start.25 = (f32[384,4,64]{0,2,1:T(8,128)S(1)}, f32[384,4,64]{0,2,1:T(8,128)}, u32[]{:S(2)}) copy-start(f32[384,4,64]{0,2,1:T(8,128)} %get-tuple-element.34) | copy-start | bytes 1179652
  227.5 3.5 %copy-start.9 = (bf16[384,2048]{1,0:T(8,128)(2,1)S(1)}, bf16[384,2048]{1,0:T(8,128)(2,1)}, u32[]{:S(2)}) copy-start(bf16[384,2048]{1,0:T(8,128)(2,1)} %param.12) | copy-start | bytes 4718596
  229.8 3.2 %copy-start.24 = (f32[384,32]{0,1:T(8,128)S(1)}, f32[384,32]{0,1:T(8,128)}, u32[]{:S(2)}) copy-start(f32[384,32]{0,1:T(8,128)} %copy-done.23) | copy-start | bytes 147460
  229.8 3.2 %copy-start.34 = (f32[384,64]{0,1:T(8,128)S(1)}, f32[384,64]{0,1:T(8,128)}, u32[]{:S(2)}) copy-start(f32[384,64]{0,1:T(8,128)} %fusion.70) | copy-start | bytes 294916
  229.8 3.2 %copy-start.31 = (f32[384,32]{0,1:T(8,128)S(1)}, f32[384,32]{0,1:T(8,128)}, u32[]{:S(2)}) copy-start(f32[384,32]{0,1:T(8,128)} %copy-done.30) | copy-start | bytes 147460
  233.0 3.3 %copy-start.28 = (bf16[2048,64]{0,1:T(8,128)(2,1)S(1)}, bf16[2048,64]{0,1:T(8,128)(2,1)}, u32[]{:S(2)}) copy-start(bf16[2048,64]{0,1:T(8,128)(2,1)} %convolution_convert_fusion.3) | copy-start | bytes 786436
  (1 other events, 0.6 us)
